TPU v7x, 32 devices: a whole 2x2x4 slice. The times are simulated.
32 devices in a mesh: cells: 8 (over z, x), genes: 4 (over y, core).
Axes of the slice: x: 2, y: 2, z: 4, core: 2. Of those that a mesh axis runs over, the one named last changes fastest.
Arguments:
- expression: bfloat16 [32768, 4096], P('cells', 'genes'), may hold values from -200 to 200
- labels: int32 [32768], P('cells'), may hold values from 0 to 199, as said below
- loadings: bfloat16 [4096, 50], P('genes'), may hold values from -0.09375 to 0.09375
Outputs:
- adjusted: bfloat16 [32768, 4096], P('cells', 'genes')
- scores: float32 [32768, 50], P('cells')
Inputs may be any that keep to these rules, and one draw needn't show every extreme that they name: `labels`: every batch has two or more cells.
All inputs are finite; a program needn't handle non-finite values.
Results may differ from a plain program's by a relative error of at most 0.0029.
Values sent between devices are 32-bit elements; how exact they have to be, the bound alone decides.
No kernel may reach another device: no remote copies, remote signals or barrier semaphores. Data moves between devices by JAX's collectives and lax.ppermute only.
A program may use at most 64 MiB of HBM per device.

v0:
```python
import math
import jax
import jax.numpy as jnp
from jax import lax
from jax.sharding import PartitionSpec as P

GENES = 4096
BATCHES = 200
SWEEPS = 10


def batch_moments(sum_one, sum_two, counts, total_cells):
    grand = jnp.sum(sum_one, axis=0) / total_cells
    within = sum_two - sum_one * sum_one / counts[:, None]
    pooled = jnp.sum(within, axis=0) / total_cells + 1e-06
    gene_sd = jnp.sqrt(pooled)
    gamma_hat = (sum_one / counts[:, None] - grand[None, :]) / gene_sd[None, :]
    delta_hat = within / ((counts[:, None] - 1.0) * pooled[None, :])
    return (grand, gene_sd, gamma_hat, delta_hat)


def gene_terms(gamma_hat, delta_hat):
    return (
        jnp.sum(gamma_hat, axis=1),
        jnp.sum(gamma_hat * gamma_hat, axis=1),
        jnp.sum(delta_hat, axis=1),
        jnp.sum(delta_hat * delta_hat, axis=1),
    )


def shrink(gamma_hat, delta_hat, counts, spread):
    sum_gamma, sum_gamma_sq, sum_delta, sum_delta_sq = spread
    gamma_bar = sum_gamma / GENES
    tau_sq = (sum_gamma_sq - GENES * gamma_bar * gamma_bar) / (GENES - 1)
    delta_mean = sum_delta / GENES
    delta_var = (sum_delta_sq - GENES * delta_mean * delta_mean) / (GENES - 1) + 1e-06
    a_prior = (2.0 * delta_var + delta_mean * delta_mean) / delta_var
    b_prior = (delta_mean * delta_var + delta_mean**3) / delta_var
    weight = counts[:, None]

    def sweep(sweep_index, state):
        gamma_now, delta_now = state
        gamma_next = (weight * tau_sq[:, None] * gamma_hat + delta_now * gamma_bar[:, None]) / (
            weight * tau_sq[:, None] + delta_now
        )
        sum_sq = (weight - 1.0) * delta_hat + weight * (gamma_hat - gamma_next) ** 2
        delta_next = (0.5 * sum_sq + b_prior[:, None]) / (0.5 * weight + a_prior[:, None] - 1.0)
        return (gamma_next, delta_next)

    gamma_star, delta_star = lax.fori_loop(0, SWEEPS, sweep, (gamma_hat, delta_hat))
    return (gamma_star, 1.0 / jnp.sqrt(delta_star))


def split_three(initial):
    upper_part = lax.optimization_barrier(initial.astype(jnp.bfloat16))
    remainder = initial - upper_part.astype(jnp.float32)
    middle_part = lax.optimization_barrier(remainder.astype(jnp.bfloat16))
    lower_part = (remainder - middle_part.astype(jnp.float32)).astype(jnp.bfloat16)
    return (upper_part, middle_part, lower_part)


def body(expression, labels, loadings):
    cell_rows, gene_cols = expression.shape
    block_rows = math.gcd(cell_rows, 1024)
    block_count = cell_rows // block_rows
    indices = jnp.arange(block_count, dtype=jnp.int32)
    batch_ids = jnp.arange(BATCHES, dtype=jnp.int32)
    total_cells = cell_rows * lax.axis_size("cells")

    def members_of(start):
        local_labels = lax.dynamic_slice_in_dim(labels, start, block_rows, 0)
        return (batch_ids[:, None] == local_labels[None, :]).astype(jnp.bfloat16)

    def accumulate(totals, block_index):
        start = block_index * block_rows
        values = lax.dynamic_slice_in_dim(expression, start, block_rows, 0)
        widened = values.astype(jnp.float32)
        square_upper, square_middle, square_lower = split_three(widened * widened)
        stacked = jnp.concatenate([values, square_upper, square_middle, square_lower], axis=1)
        members = members_of(start)
        product = jnp.dot(members, stacked, preferred_element_type=jnp.float32)
        first = product[:, :gene_cols]
        second = (
            product[:, gene_cols : 2 * gene_cols]
            + product[:, 2 * gene_cols : 3 * gene_cols]
            + product[:, 3 * gene_cols :]
        )
        number = jnp.sum(members.astype(jnp.float32), axis=1)
        return ((totals[0] + first, totals[1] + second, totals[2] + number), None)

    zeros_table = jnp.zeros((BATCHES, gene_cols), jnp.float32)
    (sum_one, sum_two, counts), unused = lax.scan(
        accumulate, (zeros_table, zeros_table, jnp.zeros((BATCHES,), jnp.float32)), indices
    )
    sum_one, sum_two, counts = lax.psum((sum_one, sum_two, counts), "cells")
    grand, gene_sd, gamma_hat, delta_hat = batch_moments(sum_one, sum_two, counts, total_cells)
    spread = lax.psum(gene_terms(gamma_hat, delta_hat), "genes")
    gamma_star, scale_star = shrink(gamma_hat, delta_hat, counts, spread)
    table_parts = split_three(jnp.concatenate([gamma_star, scale_star], axis=1))

    def adjust(block_index):
        start = block_index * block_rows
        values = lax.dynamic_slice_in_dim(expression, start, block_rows, 0).astype(jnp.float32)
        members = members_of(start)
        looked = lax.dot_general(
            members, table_parts[0], (((0,), (0,)), ((), ())), preferred_element_type=jnp.float32
        )
        looked = looked + lax.dot_general(
            members, table_parts[1], (((0,), (0,)), ((), ())), preferred_element_type=jnp.float32
        )
        looked = looked + lax.dot_general(
            members, table_parts[2], (((0,), (0,)), ((), ())), preferred_element_type=jnp.float32
        )
        shifted = (values - grand[None, :]) / gene_sd[None, :]
        standard = (shifted - looked[:, :gene_cols]) * looked[:, gene_cols:]
        adjusted = (gene_sd[None, :] * standard + grand[None, :]).astype(jnp.bfloat16)
        standard_low = standard.astype(jnp.bfloat16)
        partial_value = jnp.dot(standard_low, loadings, preferred_element_type=jnp.float32)
        return (adjusted, partial_value)

    adjusted, partial_value = lax.map(adjust, indices)
    adjusted = adjusted.reshape(cell_rows, gene_cols)
    partial_value = partial_value.reshape(cell_rows, loadings.shape[1])
    scores = lax.psum(partial_value, "genes")
    return (adjusted, scores)


def solution(mesh):
    placed = (P("cells", "genes"), P("cells"), P("genes", None))
    return jax.shard_map(
        body,
        mesh=mesh,
        in_specs=placed,
        out_specs=(P("cells", "genes"), P("cells", None)),
        check_vma=False,
    )
```

profile of v0, /device:TPU:0, one launch (start us, length us, event | category | flops | bytes accessed | tf_op | source)
XLA Modules:
  0.0 286.7 jit_solution(8608671346428369143)
XLA Ops:
  7.2 47.7 %while.45 = (s32[]{:T(128)}, f32[200,1024]{1,0:T(8,128)}, f32[200,1024]{1,0:T(8,128)}, f32[200]{0:T(256)S(1)}, s32[4]{0:T(128)S(1)}, /*index=5*/s32[4096]{0:T(10...) while((s32[]{:T(128)}, f32[200,1024]{1,0:T(8,128)}, ...), condition=%wide.region_2.3_spmd.clone, body=%wide.region_0.2_spmd.clone.sunk | while | flops 1729257600 | bytes 39210296 | solution.py:92
  8.5 2.4 fusion.69
  12.0 1.6 subtract_convert_fusion.3
  14.2 2.0 fusion.71
  16.2 1.7 fusion.72
  19.4 2.4 fusion.69
  22.8 1.6 subtract_convert_fusion.3
  25.1 2.0 fusion.71
  27.1 3.1 %fusion.72 = (f32[200,1024]{1,0:T(8,128)}, f32[200,1024]{1,0:T(8,128)}) fusion(f32[200,4096]{1,0:T(8,128)S(1)} %fusion.71, f32[200,1024]{1,0:T(8,128)} %get-tuple-element.627, pred[]{:T(512)S(6)} %compare.3, f32[200,1024]{1,0:T(8,128)} %get-tuple-element.626), kind=kLoop, calls=%fused_computation.35.clone.1 | loop fusion | flops 1228800 | bytes 6553601 | tf_op jit(solution)/shard_map/while/body/eval_jaxpr/add | solution.py:89
  31.6 2.4 fusion.69
  35.1 1.6 subtract_convert_fusion.3
  37.4 2.0 fusion.71
  39.4 3.1 %fusion.72 = (f32[200,1024]{1,0:T(8,128)}, f32[200,1024]{1,0:T(8,128)}) fusion(f32[200,4096]{1,0:T(8,128)S(1)} %fusion.71, f32[200,1024]{1,0:T(8,128)} %get-tuple-element.627, pred[]{:T(512)S(6)} %compare.3, f32[200,1024]{1,0:T(8,128)} %get-tuple-element.626), kind=kLoop, calls=%fused_computation.35.clone.1 | loop fusion | flops 1228800 | bytes 6553601 | tf_op jit(solution)/shard_map/while/body/eval_jaxpr/add | solution.py:89
  43.9 2.4 fusion.69
  47.4 1.6 subtract_convert_fusion.3
  49.6 2.0 fusion.71
  51.6 3.1 %fusion.72 = (f32[200,1024]{1,0:T(8,128)}, f32[200,1024]{1,0:T(8,128)}) fusion(f32[200,4096]{1,0:T(8,128)S(1)} %fusion.71, f32[200,1024]{1,0:T(8,128)} %get-tuple-element.627, pred[]{:T(512)S(6)} %compare.3, f32[200,1024]{1,0:T(8,128)} %get-tuple-element.626), kind=kLoop, calls=%fused_computation.35.clone.1 | loop fusion | flops 1228800 | bytes 6553601 | tf_op jit(solution)/shard_map/while/body/eval_jaxpr/add | solution.py:89
  55.0 23.9 %psum.58 = f32[200]{0:T(256)S(1)} all-reduce(f32[200]{0:T(256)S(1)} %get-tuple-element.268), channel_id=1, replica_groups=mesh['cells'=8,'genes'=4] {'cells'}, use_global_device_ids=true, to_apply=%region_4.5 | all-reduce | flops 200 | bytes 1600 | tf_op jit(solution)/shard_map/psum | solution.py:95
  78.9 70.5 %all-reduce.7.cloned.1.call-done = (f32[200,1024]{1,0:T(8,128)}, f32[200,1024]{1,0:T(8,128)}) async-done(((f32[200,1024]{1,0:T(8,128)}, f32[200,1024]{1,0:T(8,128)}), (f32[200,1024]{1,0:T(8,128)}, f32[200,1024]{1,0:T(8,128)})) %all-reduce.7.cloned.1.call-update) | async-done | bytes 1638416 | tf_op jit(solution)/shard_map/psum | solution.py:95
  149.5 1.6 fusion.39
  151.1 2.0 multiply_reduce_fusion
  154.1 7.0 %all-reduce.1 = (f32[200]{0:T(256)S(1)}, f32[200]{0:T(256)S(1)}, f32[200]{0:T(256)S(1)}, f32[200]{0:T(256)S(1)}) all-reduce(f32[200]{0:T(256)S(1)} %get-tuple-element.407, f32[200]{0:T(256)S(1)} %get-tuple-element.408, f32[200]{0:T(256)S(1)} %get-tuple-element.326, ...), channel_id=1, replica_groups=mesh['cells'=8,'genes'=4] {'genes'}, use_global_device_ids=true, to_apply=%region_15.16 | all-reduce | flops 800 | bytes 6400 | tf_op jit(solution)/shard_map/psum | solution.py:97
  161.1 13.3 %while.43 = (s32[]{:T(128)}, f32[200,1024]{1,0:T(8,128)}, f32[200,1024]{1,0:T(8,128)S(1)}, f32[200,1]{0,1:T(1,128)S(1)}, f32[200,1024]{1,0:T(8,128)S(1)}, /*inde...) while((s32[]{:T(128)}, f32[200,1024]{1,0:T(8,128)}, ...), condition=%wide.region_17.18_spmd, body=%wide.region_16.17_spmd.sunk | while | flops 2663202 | bytes 4104109 | solution.py:50
  161.1 1.3 add_divide_fusion.5
  162.5 1.3 add_divide_fusion.5
  163.8 1.3 add_divide_fusion.5
  165.1 1.3 add_divide_fusion.5
  166.5 1.3 add_divide_fusion.5
  169.1 1.3 add_divide_fusion.5
  170.5 1.3 add_divide_fusion.5
  171.8 1.3 add_divide_fusion.5
  173.1 1.3 add_divide_fusion.5
  176.8 63.9 %while.44 = (s32[]{:T(128)}, bf16[4,1024,1024]{2,1,0:T(8,128)(2,1)}, f32[4,1024,50]{1,0,2:T(4,128)}, f32[1024]{0:T(1024)S(1)}, s32[4]{0:T(128)S(1)}, /*index=5*/...) while((s32[]{:T(128)}, ...), condition=%wide.region_19.20_spmd.clone, body=%wide.region_18.19_spmd.clone.sunk | while | flops 2635685888 | bytes 62333656 | solution.py:121
  181.5 1.5 add_add_fusion.3
  183.0 3.7 %fusion.66 = (bf16[4,1024,1024]{2,1,0:T(8,128)(2,1)}, bf16[1024,1024]{1,0:T(8,128)(2,1)S(1)}) fusion(bf16[4,1024,1024]{2,1,0:T(8,128)(2,1)} %get-tuple-element.697, s32[]{:T(128)} %get-tuple-element.696, f32[1024]{0:T(1024)S(1)} %get-tuple-element.718, f32[1024]{0:T(1024)S(1)} %get-tuple-element.715, f32[1024,2048]{1,0:T(8,128)S(1)} %add_add_fusion.3, ...), kind=kLoop, calls=%fused_computation.11.clone.1 | loop fusion | flops 9437184 | bytes 14688772 | tf_op jit(solution)/shard_map/while/body/jit(dynamic_update_index_in_dim)/dynamic_update_slice | solution.py:121
  187.7 5.1 %dynamic_update_slice.14 = f32[4,1024,50]{1,0,2:T(4,128)} dynamic-update-slice(f32[4,1024,50]{1,0,2:T(4,128)} %get-tuple-element.698, f32[1,1024,50]{1,0,2:T(1,128)S(1)} %copy.17, s32[]{:T(128)} %get-tuple-element.696, s32[]{:T(128)} %constant.76.clone.1..sunk, s32[]{:T(128)} %constant.76.clone.1..sunk) | dynamic-update-slice | bytes 409604 | tf_op jit(solution)/shard_map/while/body/jit(dynamic_update_index_in_dim)/dynamic_update_slice | solution.py:121
  197.5 1.5 add_add_fusion.3
  199.0 3.7 %fusion.66 = (bf16[4,1024,1024]{2,1,0:T(8,128)(2,1)}, bf16[1024,1024]{1,0:T(8,128)(2,1)S(1)}) fusion(bf16[4,1024,1024]{2,1,0:T(8,128)(2,1)} %get-tuple-element.697, s32[]{:T(128)} %get-tuple-element.696, f32[1024]{0:T(1024)S(1)} %get-tuple-element.718, f32[1024]{0:T(1024)S(1)} %get-tuple-element.715, f32[1024,2048]{1,0:T(8,128)S(1)} %add_add_fusion.3, ...), kind=kLoop, calls=%fused_computation.11.clone.1 | loop fusion | flops 9437184 | bytes 14688772 | tf_op jit(solution)/shard_map/while/body/jit(dynamic_update_index_in_dim)/dynamic_update_slice | solution.py:121
  203.7 5.1 %dynamic_update_slice.14 = f32[4,1024,50]{1,0,2:T(4,128)} dynamic-update-slice(f32[4,1024,50]{1,0,2:T(4,128)} %get-tuple-element.698, f32[1,1024,50]{1,0,2:T(1,128)S(1)} %copy.17, s32[]{:T(128)} %get-tuple-element.696, s32[]{:T(128)} %constant.76.clone.1..sunk, s32[]{:T(128)} %constant.76.clone.1..sunk) | dynamic-update-slice | bytes 409604 | tf_op jit(solution)/shard_map/while/body/jit(dynamic_update_index_in_dim)/dynamic_update_slice | solution.py:121
  213.4 1.5 add_add_fusion.3
  214.9 3.7 %fusion.66 = (bf16[4,1024,1024]{2,1,0:T(8,128)(2,1)}, bf16[1024,1024]{1,0:T(8,128)(2,1)S(1)}) fusion(bf16[4,1024,1024]{2,1,0:T(8,128)(2,1)} %get-tuple-element.697, s32[]{:T(128)} %get-tuple-element.696, f32[1024]{0:T(1024)S(1)} %get-tuple-element.718, f32[1024]{0:T(1024)S(1)} %get-tuple-element.715, f32[1024,2048]{1,0:T(8,128)S(1)} %add_add_fusion.3, ...), kind=kLoop, calls=%fused_computation.11.clone.1 | loop fusion | flops 9437184 | bytes 14688772 | tf_op jit(solution)/shard_map/while/body/jit(dynamic_update_index_in_dim)/dynamic_update_slice | solution.py:121
  219.6 5.1 %dynamic_update_slice.14 = f32[4,1024,50]{1,0,2:T(4,128)} dynamic-update-slice(f32[4,1024,50]{1,0,2:T(4,128)} %get-tuple-element.698, f32[1,1024,50]{1,0,2:T(1,128)S(1)} %copy.17, s32[]{:T(128)} %get-tuple-element.696, s32[]{:T(128)} %constant.76.clone.1..sunk, s32[]{:T(128)} %constant.76.clone.1..sunk) | dynamic-update-slice | bytes 409604 | tf_op jit(solution)/shard_map/while/body/jit(dynamic_update_index_in_dim)/dynamic_update_slice | solution.py:121
  229.4 1.5 add_add_fusion.3
  230.9 3.7 %fusion.66 = (bf16[4,1024,1024]{2,1,0:T(8,128)(2,1)}, bf16[1024,1024]{1,0:T(8,128)(2,1)S(1)}) fusion(bf16[4,1024,1024]{2,1,0:T(8,128)(2,1)} %get-tuple-element.697, s32[]{:T(128)} %get-tuple-element.696, f32[1024]{0:T(1024)S(1)} %get-tuple-element.718, f32[1024]{0:T(1024)S(1)} %get-tuple-element.715, f32[1024,2048]{1,0:T(8,128)S(1)} %add_add_fusion.3, ...), kind=kLoop, calls=%fused_computation.11.clone.1 | loop fusion | flops 9437184 | bytes 14688772 | tf_op jit(solution)/shard_map/while/body/jit(dynamic_update_index_in_dim)/dynamic_update_slice | solution.py:121
  235.6 5.1 %dynamic_update_slice.14 = f32[4,1024,50]{1,0,2:T(4,128)} dynamic-update-slice(f32[4,1024,50]{1,0,2:T(4,128)} %get-tuple-element.698, f32[1,1024,50]{1,0,2:T(1,128)S(1)} %copy.17, s32[]{:T(128)} %get-tuple-element.696, s32[]{:T(128)} %constant.76.clone.1..sunk, s32[]{:T(128)} %constant.76.clone.1..sunk) | dynamic-update-slice | bytes 409604 | tf_op jit(solution)/shard_map/while/body/jit(dynamic_update_index_in_dim)/dynamic_update_slice | solution.py:121
  242.0 1.5 copy.15
  243.5 34.2 %all-reduce.5.cloned.1.call-done = f32[4096,50]{0,1:T(8,128)} async-done(((f32[4096,50]{0,1:T(8,128)}), f32[4096,50]{0,1:T(8,128)}) %all-reduce.5.cloned.1.call-update) | async-done | bytes 819216 | tf_op jit(solution)/shard_map/psum | solution.py:124
  277.7 2.2 copy.53
  (81 shorter events, 35.8 us)
Async XLA Ops:
  7.2 142.3 %all-reduce.7.cloned.1.call-start = ((), (), s32[]{:S(2)}) async-start(), calls=%async_computation.1 | async-start | bytes 3276800 | tf_op jit(solution)/shard_map/psum | solution.py:95
  54.9 222.7 %all-reduce.5.cloned.1.call-start = ((), (), s32[]{:S(2)}) async-start(), calls=%async_computation | async-start | bytes 1835008 | tf_op jit(solution)/shard_map/psum | solution.py:124
  174.4 1.4 copy-start
  175.9 0.9 copy-start.1
Sparse Core Ops, SparseCore 0:
  55.1 94.3 all-reduce.6
  243.6 34.0 all-reduce.4
where the time goes:
time: 288 us; the launch traced here: 287 us
  waiting for transfers between devices  105 us (36%)
  other arithmetic  65.5 us (23%)
  local copies, waits for them, and re-layouts  38 us (13%)
  blocking collectives  30.9 us (11%)
  matrix products  27.6 us (10%)
  between operations  14.2 us (5%)
  loops' own time  5.76 us (2%)
    psum x1, waiting for transfers between devices, body(): sum_one, sum_two, counts = lax.psum((sum_one, sum_two, counts), 'cells')  70.5 us
    psum x1, waiting for transfers between devices, body(): scores = lax.psum(partial_value, 'genes')  34.2 us
    psum x1, blocking collectives, body(): sum_one, sum_two, counts = lax.psum((sum_one, sum_two, counts), 'cells')  23.9 us
    dynamic_update_slice x8, local copies, waits for them, and re-layouts, body(): adjusted, partial_value = lax.map(adjust, indices)  21.1 us
    dynamic_update_slice x4, other arithmetic, body(): adjusted, partial_value = lax.map(adjust, indices)  14.9 us
    div x10, other arithmetic, sweep(): (0.5 * sum_sq + b_prior[:, None]) / (0.5 * weight + a_prior[:, None] - 1.0)  13.2 us
    convert_element_type x5, other arithmetic, split_three(): upper_part = lax.optimization_barrier(initial.astype(jnp.bfloat16))  11.1 us
    add x8, other arithmetic, accumulate(): return ((totals[0] + first, totals[1] + second, totals[2] + number), None)  11 us
  transfers between devices with their start and end apart: 2, of which 2 were waited for; matrix products, arithmetic and copies ran while one was open for 0% of the time, Pallas kernels for 0%

commit v1 on v0

--- a/solution.py
+++ b/solution.py
@@ -121,7 +121,9 @@
     adjusted, partial_value = lax.map(adjust, indices)
     adjusted = adjusted.reshape(cell_rows, gene_cols)
     partial_value = partial_value.reshape(cell_rows, loadings.shape[1])
-    scores = lax.psum(partial_value, "genes")
+    scores = partial_value
+    for hop in (1, 2):
+        scores = scores + lax.ppermute(scores, "genes", [(dev, dev ^ hop) for dev in range(4)])
     return (adjusted, scores)
 
 

time: 288 us -> 277 us (0.962)
  waiting for transfers between devices: 105 us -> 95 us
  local copies, waits for them, and re-layouts: 38 us -> 34.9 us
    psum x1 -> x0, waiting for transfers between devices: 34.2 us -> none  [body(): scores = lax.psum(partial_value, 'genes')]
    ppermute x0 -> x2, waiting for transfers between devices: none -> 24.3 us  [body(): lax.ppermute(scores, 'genes', [(dev, dev ^ hop) for dev in range(4)])]
    unnamed x9 -> x8, local copies, waits for them, and re-layouts: 6.15 us -> 3.07 us
  transfers between devices with their start and end apart: 2 -> 3, of which waited for: 2 -> 3; matrix products, arithmetic and copies ran while one was open for 0% -> 0% of each run, Pallas kernels for 0% -> 0%
where the time goes in v1:
time: 277 us; the launch traced here: 276 us
  waiting for transfers between devices  95 us (34%)
  other arithmetic  66.6 us (24%)
  local copies, waits for them, and re-layouts  34.9 us (13%)
  blocking collectives  30.9 us (11%)
  matrix products  27.6 us (10%)
  between operations  14.2 us (5%)
  loops' own time  5.76 us (2%)
    psum x1, waiting for transfers between devices, body(): sum_one, sum_two, counts = lax.psum((sum_one, sum_two, counts), 'cells')  70.7 us
    ppermute x2, waiting for transfers between devices, body(): lax.ppermute(scores, 'genes', [(dev, dev ^ hop) for dev in range(4)])  24.3 us
    psum x1, blocking collectives, body(): sum_one, sum_two, counts = lax.psum((sum_one, sum_two, counts), 'cells')  23.8 us
    dynamic_update_slice x8, local copies, waits for them, and re-layouts, body(): adjusted, partial_value = lax.map(adjust, indices)  21.1 us
    dynamic_update_slice x4, other arithmetic, body(): adjusted, partial_value = lax.map(adjust, indices)  14.9 us
    div x10, other arithmetic, sweep(): (0.5 * sum_sq + b_prior[:, None]) / (0.5 * weight + a_prior[:, None] - 1.0)  13.2 us
    convert_element_type x5, other arithmetic, split_three(): upper_part = lax.optimization_barrier(initial.astype(jnp.bfloat16))  11.1 us
    add x8, other arithmetic, accumulate(): return ((totals[0] + first, totals[1] + second, totals[2] + number), None)  11 us
  transfers between devices with their start and end apart: 3, of which 3 were waited for; matrix products, arithmetic and copies ran while one was open for 0% of the time, Pallas kernels for 0%

profile of v1, /device:TPU:0, one launch (start us, length us, event | category | flops | bytes accessed | tf_op | source)
XLA Modules:
  0.0 275.5 jit_solution(4019044979243054919)
XLA Ops:
  7.2 47.7 %while.45 = (s32[]{:T(128)}, f32[200,1024]{1,0:T(8,128)}, f32[200,1024]{1,0:T(8,128)}, f32[200]{0:T(256)S(1)}, s32[4]{0:T(128)S(1)}, /*index=5*/s32[4096]{0:T(10...) while((s32[]{:T(128)}, f32[200,1024]{1,0:T(8,128)}, ...), condition=%wide.region_2.3_spmd.clone, body=%wide.region_0.2_spmd.clone.sunk | while | flops 1729257600 | bytes 39210296 | solution.py:92
  8.5 2.4 fusion.69
  12.0 1.6 subtract_convert_fusion.3
  14.2 2.0 fusion.71
  16.2 1.7 fusion.72
  19.4 2.4 fusion.69
  22.8 1.6 subtract_convert_fusion.3
  25.1 2.0 fusion.71
  27.1 3.1 %fusion.72 = (f32[200,1024]{1,0:T(8,128)}, f32[200,1024]{1,0:T(8,128)}) fusion(f32[200,4096]{1,0:T(8,128)S(1)} %fusion.71, f32[200,1024]{1,0:T(8,128)} %get-tuple-element.627, pred[]{:T(512)S(6)} %compare.3, f32[200,1024]{1,0:T(8,128)} %get-tuple-element.626), kind=kLoop, calls=%fused_computation.35.clone.1 | loop fusion | flops 1228800 | bytes 6553601 | tf_op jit(solution)/shard_map/while/body/eval_jaxpr/add | solution.py:89
  31.6 2.4 fusion.69
  35.1 1.6 subtract_convert_fusion.3
  37.4 2.0 fusion.71
  39.4 3.1 %fusion.72 = (f32[200,1024]{1,0:T(8,128)}, f32[200,1024]{1,0:T(8,128)}) fusion(f32[200,4096]{1,0:T(8,128)S(1)} %fusion.71, f32[200,1024]{1,0:T(8,128)} %get-tuple-element.627, pred[]{:T(512)S(6)} %compare.3, f32[200,1024]{1,0:T(8,128)} %get-tuple-element.626), kind=kLoop, calls=%fused_computation.35.clone.1 | loop fusion | flops 1228800 | bytes 6553601 | tf_op jit(solution)/shard_map/while/body/eval_jaxpr/add | solution.py:89
  43.9 2.4 fusion.69
  47.4 1.6 subtract_convert_fusion.3
  49.6 2.0 fusion.71
  51.6 3.1 %fusion.72 = (f32[200,1024]{1,0:T(8,128)}, f32[200,1024]{1,0:T(8,128)}) fusion(f32[200,4096]{1,0:T(8,128)S(1)} %fusion.71, f32[200,1024]{1,0:T(8,128)} %get-tuple-element.627, pred[]{:T(512)S(6)} %compare.3, f32[200,1024]{1,0:T(8,128)} %get-tuple-element.626), kind=kLoop, calls=%fused_computation.35.clone.1 | loop fusion | flops 1228800 | bytes 6553601 | tf_op jit(solution)/shard_map/while/body/eval_jaxpr/add | solution.py:89
  55.0 23.8 %psum.51 = f32[200]{0:T(256)S(1)} all-reduce(f32[200]{0:T(256)S(1)} %get-tuple-element.268), channel_id=1, replica_groups=mesh['cells'=8,'genes'=4] {'cells'}, use_global_device_ids=true, to_apply=%region_4.5 | all-reduce | flops 200 | bytes 1600 | tf_op jit(solution)/shard_map/psum | solution.py:95
  78.8 70.7 %all-reduce.4.cloned.1.call-done = (f32[200,1024]{1,0:T(8,128)}, f32[200,1024]{1,0:T(8,128)}) async-done(((f32[200,1024]{1,0:T(8,128)}, f32[200,1024]{1,0:T(8,128)}), (f32[200,1024]{1,0:T(8,128)}, f32[200,1024]{1,0:T(8,128)})) %all-reduce.4.cloned.1.call-update) | async-done | bytes 1638416 | tf_op jit(solution)/shard_map/psum | solution.py:95
  149.5 1.6 fusion.39
  151.1 2.0 multiply_reduce_fusion
  154.1 7.0 %all-reduce.1 = (f32[200]{0:T(256)S(1)}, f32[200]{0:T(256)S(1)}, f32[200]{0:T(256)S(1)}, f32[200]{0:T(256)S(1)}) all-reduce(f32[200]{0:T(256)S(1)} %get-tuple-element.407, f32[200]{0:T(256)S(1)} %get-tuple-element.408, f32[200]{0:T(256)S(1)} %get-tuple-element.326, ...), channel_id=1, replica_groups=mesh['cells'=8,'genes'=4] {'genes'}, use_global_device_ids=true, to_apply=%region_15.16 | all-reduce | flops 800 | bytes 6400 | tf_op jit(solution)/shard_map/psum | solution.py:97
  161.1 13.3 %while.43 = (s32[]{:T(128)}, f32[200,1024]{1,0:T(8,128)}, f32[200,1024]{1,0:T(8,128)S(1)}, f32[200,1]{0,1:T(1,128)S(1)}, f32[200,1024]{1,0:T(8,128)S(1)}, /*inde...) while((s32[]{:T(128)}, f32[200,1024]{1,0:T(8,128)}, ...), condition=%wide.region_17.18_spmd, body=%wide.region_16.17_spmd.sunk | while | flops 2663202 | bytes 4104109 | solution.py:50
  161.1 1.3 add_divide_fusion.5
  162.5 1.3 add_divide_fusion.5
  163.8 1.3 add_divide_fusion.5
  165.1 1.3 add_divide_fusion.5
  166.5 1.3 add_divide_fusion.5
  167.8 1.3 add_divide_fusion.5
  169.1 1.3 add_divide_fusion.5
  170.5 1.3 add_divide_fusion.5
  171.8 1.3 add_divide_fusion.5
  173.1 1.3 add_divide_fusion.5
  176.8 63.9 %while.44 = (s32[]{:T(128)}, bf16[4,1024,1024]{2,1,0:T(8,128)(2,1)}, f32[4,1024,50]{1,0,2:T(4,128)}, f32[1024]{0:T(1024)S(1)}, s32[4]{0:T(128)S(1)}, /*index=5*/...) while((s32[]{:T(128)}, ...), condition=%wide.region_19.20_spmd.clone, body=%wide.region_18.19_spmd.clone.sunk | while | flops 2635685888 | bytes 62333656 | solution.py:121
  181.5 1.5 add_add_fusion.3
  183.0 3.7 %fusion.66 = (bf16[4,1024,1024]{2,1,0:T(8,128)(2,1)}, bf16[1024,1024]{1,0:T(8,128)(2,1)S(1)}) fusion(bf16[4,1024,1024]{2,1,0:T(8,128)(2,1)} %get-tuple-element.697, s32[]{:T(128)} %get-tuple-element.696, f32[1024]{0:T(1024)S(1)} %get-tuple-element.718, f32[1024]{0:T(1024)S(1)} %get-tuple-element.715, f32[1024,2048]{1,0:T(8,128)S(1)} %add_add_fusion.3, ...), kind=kLoop, calls=%fused_computation.11.clone.1 | loop fusion | flops 9437184 | bytes 14688772 | tf_op jit(solution)/shard_map/while/body/jit(dynamic_update_index_in_dim)/dynamic_update_slice | solution.py:121
  187.7 5.1 %dynamic_update_slice.14 = f32[4,1024,50]{1,0,2:T(4,128)} dynamic-update-slice(f32[4,1024,50]{1,0,2:T(4,128)} %get-tuple-element.698, f32[1,1024,50]{1,0,2:T(1,128)S(1)} %copy.17, s32[]{:T(128)} %get-tuple-element.696, s32[]{:T(128)} %constant.76.clone.1..sunk, s32[]{:T(128)} %constant.76.clone.1..sunk) | dynamic-update-slice | bytes 409604 | tf_op jit(solution)/shard_map/while/body/jit(dynamic_update_index_in_dim)/dynamic_update_slice | solution.py:121
  197.5 1.5 add_add_fusion.3
  199.0 3.7 %fusion.66 = (bf16[4,1024,1024]{2,1,0:T(8,128)(2,1)}, bf16[1024,1024]{1,0:T(8,128)(2,1)S(1)}) fusion(bf16[4,1024,1024]{2,1,0:T(8,128)(2,1)} %get-tuple-element.697, s32[]{:T(128)} %get-tuple-element.696, f32[1024]{0:T(1024)S(1)} %get-tuple-element.718, f32[1024]{0:T(1024)S(1)} %get-tuple-element.715, f32[1024,2048]{1,0:T(8,128)S(1)} %add_add_fusion.3, ...), kind=kLoop, calls=%fused_computation.11.clone.1 | loop fusion | flops 9437184 | bytes 14688772 | tf_op jit(solution)/shard_map/while/body/jit(dynamic_update_index_in_dim)/dynamic_update_slice | solution.py:121
  203.7 5.1 %dynamic_update_slice.14 = f32[4,1024,50]{1,0,2:T(4,128)} dynamic-update-slice(f32[4,1024,50]{1,0,2:T(4,128)} %get-tuple-element.698, f32[1,1024,50]{1,0,2:T(1,128)S(1)} %copy.17, s32[]{:T(128)} %get-tuple-element.696, s32[]{:T(128)} %constant.76.clone.1..sunk, s32[]{:T(128)} %constant.76.clone.1..sunk) | dynamic-update-slice | bytes 409604 | tf_op jit(solution)/shard_map/while/body/jit(dynamic_update_index_in_dim)/dynamic_update_slice | solution.py:121
  213.4 1.5 add_add_fusion.3
  214.9 3.7 %fusion.66 = (bf16[4,1024,1024]{2,1,0:T(8,128)(2,1)}, bf16[1024,1024]{1,0:T(8,128)(2,1)S(1)}) fusion(bf16[4,1024,1024]{2,1,0:T(8,128)(2,1)} %get-tuple-element.697, s32[]{:T(128)} %get-tuple-element.696, f32[1024]{0:T(1024)S(1)} %get-tuple-element.718, f32[1024]{0:T(1024)S(1)} %get-tuple-element.715, f32[1024,2048]{1,0:T(8,128)S(1)} %add_add_fusion.3, ...), kind=kLoop, calls=%fused_computation.11.clone.1 | loop fusion | flops 9437184 | bytes 14688772 | tf_op jit(solution)/shard_map/while/body/jit(dynamic_update_index_in_dim)/dynamic_update_slice | solution.py:121
  219.6 5.1 %dynamic_update_slice.14 = f32[4,1024,50]{1,0,2:T(4,128)} dynamic-update-slice(f32[4,1024,50]{1,0,2:T(4,128)} %get-tuple-element.698, f32[1,1024,50]{1,0,2:T(1,128)S(1)} %copy.17, s32[]{:T(128)} %get-tuple-element.696, s32[]{:T(128)} %constant.76.clone.1..sunk, s32[]{:T(128)} %constant.76.clone.1..sunk) | dynamic-update-slice | bytes 409604 | tf_op jit(solution)/shard_map/while/body/jit(dynamic_update_index_in_dim)/dynamic_update_slice | solution.py:121
  229.4 1.5 add_add_fusion.3
  230.9 3.7 %fusion.66 = (bf16[4,1024,1024]{2,1,0:T(8,128)(2,1)}, bf16[1024,1024]{1,0:T(8,128)(2,1)S(1)}) fusion(bf16[4,1024,1024]{2,1,0:T(8,128)(2,1)} %get-tuple-element.697, s32[]{:T(128)} %get-tuple-element.696, f32[1024]{0:T(1024)S(1)} %get-tuple-element.718, f32[1024]{0:T(1024)S(1)} %get-tuple-element.715, f32[1024,2048]{1,0:T(8,128)S(1)} %add_add_fusion.3, ...), kind=kLoop, calls=%fused_computation.11.clone.1 | loop fusion | flops 9437184 | bytes 14688772 | tf_op jit(solution)/shard_map/while/body/jit(dynamic_update_index_in_dim)/dynamic_update_slice | solution.py:121
  235.6 5.1 %dynamic_update_slice.14 = f32[4,1024,50]{1,0,2:T(4,128)} dynamic-update-slice(f32[4,1024,50]{1,0,2:T(4,128)} %get-tuple-element.698, f32[1,1024,50]{1,0,2:T(1,128)S(1)} %copy.17, s32[]{:T(128)} %get-tuple-element.696, s32[]{:T(128)} %constant.76.clone.1..sunk, s32[]{:T(128)} %constant.76.clone.1..sunk) | dynamic-update-slice | bytes 409604 | tf_op jit(solution)/shard_map/while/body/jit(dynamic_update_index_in_dim)/dynamic_update_slice | solution.py:121
  242.6 2.5 collective-permute-done
  245.8 21.8 %collective-permute-done.1 = f32[4096,50]{0,1:T(8,128)S(1)} collective-permute-done((f32[4096,50]{0,1:T(8,128)S(1)}, f32[4096,50]{0,1:T(8,128)S(1)}, u32[]{:S(2)}, u32[]{:S(2)}) %collective-permute-start.1) | collective-permute-done | bytes 819232 | tf_op jit(solution)/shard_map/ppermute | solution.py:126
  (83 shorter events, 36.7 us)
Async XLA Ops:
  7.2 142.3 %all-reduce.4.cloned.1.call-start = ((), (), s32[]{:S(2)}) async-start(), calls=%async_computation | async-start | bytes 3276800 | tf_op jit(solution)/shard_map/psum | solution.py:95
  174.4 1.4 copy-start
  175.9 0.9 copy-start.1
  242.6 2.5 collective-permute-start
  245.2 22.5 %collective-permute-start.1 = (f32[4096,50]{0,1:T(8,128)S(1)}, f32[4096,50]{0,1:T(8,128)S(1)}, u32[]{:S(2)}, u32[]{:S(2)}) collective-permute-start(f32[4096,50]{0,1:T(8,128)S(1)} %add.173), channel_id=1, source_target_pairs={{0,2},{1,3},{2,0},{3,1},{4,6},{5,7},{6,4},{7,5},{8,10},{9,11},{10,... | collective-permute-start | bytes 2457608 | tf_op jit(solution)/shard_map/ppermute | solution.py:126
Sparse Core Ops, SparseCore 0:
  55.1 94.3 all-reduce.3
